TPU v7x, 128 devices: a whole 4x4x4 slice. The times are simulated.
128 devices in a mesh: rows: 8 (over z, core), cols: 4 (over x), slabs: 4 (over y).
Axes of the slice: x: 4, y: 4, z: 4, core: 2. Of those that a mesh axis runs over, the one named last changes fastest.
Arguments:
- field_now: float32 [32, 128, 512, 128], P('rows', 'cols', 'slabs'), may hold values from 0.5 to 2
- earlier: float32 [32, 128, 512, 128], P('rows', 'cols', 'slabs'), may hold values from 0.2 to 1.8
- speed_square: float32 [32, 128, 512, 128], P('rows', 'cols', 'slabs'), may hold values from 0.05 to 0.3
Outputs:
- scaled_field: float32 [32, 128, 512, 128], P('rows', 'cols', 'slabs')
- field_now_end: float32 [32, 128, 512, 128], P('rows', 'cols', 'slabs')
All inputs are finite; a program needn't handle non-finite values.
Results may differ from a plain program's by a relative error of at most 0.00002.
Values sent between devices are 32-bit elements; how exact they have to be, the bound alone decides.
A program may use at most 128 MiB of HBM per device.

v0:
```python
import jax
import jax.numpy as jnp
from jax import lax
from jax.sharding import PartitionSpec as P

STEPS = 3


def extended(value, sides, width):
    edges = {}
    for axis, dim in sides:
        size, length = (lax.axis_size(axis), value.shape[dim])
        up = [(i, (i + 1) % size) for i in range(size - 1)]
        last = lax.slice_in_dim(value, length - width, length, axis=dim)
        leading = lax.slice_in_dim(value, 0, width, axis=dim)
        edges[dim] = (
            lax.ppermute(last, axis, up),
            lax.ppermute(leading, axis, [(b, a) for a, b in up]),
        )
    done = []
    for _, dim in sides:
        low, high = edges[dim]
        around = [(width, width) if d in done else (0, 0) for d in range(value.ndim)]
        value = jnp.concatenate([jnp.pad(low, around), value, jnp.pad(high, around)], axis=dim)
        done.append(dim)
    return value


def sent_to_all(value, axis):
    length = lax.axis_size(axis)
    return lax.all_to_all(
        jnp.broadcast_to(value[None], (length, *value.shape)), axis, 0, 0, tiled=True
    )


def taken_together(value, axis):
    everything = sent_to_all(value, axis)
    return jnp.sum(everything, axis=0)


def packed_total(arrays, axis):
    ends = [0]
    for a in arrays:
        ends.append(ends[-1] + a.size)
    so_far = taken_together(jnp.concatenate([a.ravel() for a in arrays]), axis)
    return tuple((so_far[b:e].reshape(a.shape) for a, b, e in zip(arrays, ends, ends[1:])))


def without_rim(values, dims):
    for dim in dims:
        values = lax.slice_in_dim(values, 1, values.shape[dim] - 1, axis=dim)
    return values


def shifted_cells(values, dim, start, dims):
    others = [other for other in dims if other != dim]
    values = without_rim(values, others)
    return lax.slice_in_dim(values, start, start + values.shape[dim] - 2, axis=dim)


def march_step(padded, before, speed_square):
    middle = without_rim(padded, (0, 1, 2))
    lower = [shifted_cells(padded, dim, 0, (0, 1, 2)) for dim in (0, 1, 2)]
    upper = [shifted_cells(padded, dim, 2, (0, 1, 2)) for dim in (0, 1, 2)]
    spread = lower[0] + upper[0] + lower[1] + upper[1] + lower[2] + upper[2] - 6.0 * middle
    return 2.0 * middle - before + speed_square * spread


def shards(field_now, earlier, speed_square):
    for step in range(STEPS):
        padded = extended(field_now, (("rows", 0), ("cols", 1), ("slabs", 2)), 1)
        later = march_step(padded, earlier, speed_square)
        earlier, field_now = (field_now, later)
    count = field_now.shape[2] * lax.axis_size("slabs")
    guess = 1.0
    moved = field_now - guess
    totals, squares = packed_total(
        (jnp.sum(moved, axis=2, keepdims=True), jnp.sum(moved * moved, axis=2, keepdims=True)),
        "slabs",
    )
    line_mean = guess + totals / count
    centred = field_now - line_mean
    line_variance = squares / count - totals / count * (totals / count)
    scaled_field = centred * lax.rsqrt(line_variance + 0.0001)
    return (scaled_field, field_now)


def solution(mesh):
    placed = (
        P("rows", "cols", "slabs", None),
        P("rows", "cols", "slabs", None),
        P("rows", "cols", "slabs", None),
    )
    return jax.shard_map(
        shards,
        mesh=mesh,
        in_specs=placed,
        out_specs=(P("rows", "cols", "slabs", None), P("rows", "cols", "slabs", None)),
        check_vma=False,
    )
```

profile of v0, /device:TPU:1, one launch (start us, length us, event | category | flops | bytes accessed | tf_op | source)
XLA Modules:
  0.0 206.0 jit_solution(15246103260882619323)
XLA Ops:
  0.6 2.6 %fusion.43 = (f32[1,32,128,128]{3,2,1,0:T(8,128)S(1)}, f32[1,32,128,128]{3,2,1,0:T(8,128)S(1)}) fusion(f32[4,32,128,128]{3,2,1,0:T(8,128)} %param.3), kind=kLoop, calls=%fused_computation.99 | loop fusion | bytes 8388608 | tf_op jit(solution)/shard_map/slice | solution.py:15
  3.3 5.2 %collective-permute-start = (f32[1,32,128,128]{3,2,1,0:T(8,128)S(1)}, f32[1,32,128,128]{3,2,1,0:T(8,128)S(1)}, u32[]{:S(2)}, u32[]{:S(2)}) collective-permute-start(f32[1,32,128,128]{3,2,1,0:T(8,128)S(1)} %get-tuple-element.22), channel_id=1, source_target_pairs={{0,16},{16,32},{32,48},{48,64},{64,80},{80,96},{96,112},{1,17},{17... | collective-permute-start | bytes 6291464 | tf_op jit(solution)/shard_map/ppermute | solution.py:17
  10.5 3.1 %collective-permute-start.2 = (f32[4,1,128,128]{3,2,1,0:T(8,128)S(1)}, f32[4,1,128,128]{3,2,1,0:T(8,128)S(1)}, u32[]{:S(2)}, u32[]{:S(2)}) collective-permute-start(f32[4,1,128,128]{3,2,1,0:T(8,128)S(1)} %get-tuple-element.19), channel_id=1, source_target_pairs={{0,4},{4,8},{8,12},{1,5},{5,9},{9,13},{2,6},{6,10},{10,14},{3,7},{... | collective-permute-start | bytes 786440 | tf_op jit(solution)/shard_map/ppermute | solution.py:17
  15.0 3.2 %collective-permute-start.4 = (f32[4,32,1,128]{3,2,1,0:T(1,128)S(1)}, f32[4,32,1,128]{3,2,1,0:T(1,128)S(1)}, u32[]{:S(2)}, u32[]{:S(2)}) collective-permute-start(f32[4,32,1,128]{3,2,1,0:T(1,128)S(1)} %get-tuple-element.17), channel_id=1, source_target_pairs={{0,1},{1,2},{2,3},{4,5},{5,6},{6,7},{8,9},{9,10},{10,11},{12,13},{... | collective-permute-start | bytes 196616 | tf_op jit(solution)/shard_map/ppermute | solution.py:17
  19.6 2.8 %collective-permute-done.3 = f32[4,1,128,128]{3,2,1,0:T(8,128)S(1)} collective-permute-done((f32[4,1,128,128]{3,2,1,0:T(8,128)S(1)}, f32[4,1,128,128]{3,2,1,0:T(8,128)S(1)}, u32[]{:S(2)}, u32[]{:S(2)}) %collective-permute-start.3) | collective-permute-done | bytes 262176 | tf_op jit(solution)/shard_map/ppermute | solution.py:18
  22.4 9.0 %collective-permute-done = f32[1,32,128,128]{3,2,1,0:T(8,128)S(1)} collective-permute-done((f32[1,32,128,128]{3,2,1,0:T(8,128)S(1)}, f32[1,32,128,128]{3,2,1,0:T(8,128)S(1)}, u32[]{:S(2)}, u32[]{:S(2)}) %collective-permute-start) | collective-permute-done | bytes 2097184 | tf_op jit(solution)/shard_map/ppermute | solution.py:17
  32.9 4.0 %constant_dynamic-update-slice_fusion.1 = f32[6,32,128,128]{3,2,1,0:T(8,128)} fusion(f32[6,32,128,128]{3,2,1,0:T(8,128)} %constant_dynamic-update-slice_fusion.2, f32[4,32,128,128]{3,2,1,0:T(8,128)S(1)} %copy-done), kind=kLoop, calls=%fused_computation.89 | loop fusion | bytes 16777216
  39.7 22.1 %fusion.24 = f32[4,32,128,128]{3,2,1,0:T(8,128)} fusion(f32[4,32,128,128]{3,2,1,0:T(8,128)} %param.5, f32[4,32,1,128]{3,2,1,0:T(1,128)S(1)} %collective-permute-done.5, f32[6,1,128,128]{3,2,1,0:T(8,128)S(1)} %pad.39, f32[6,32,128,128]{3,2,1,0:T(8,128)} %constant_dynamic-update-slice_fusion, f32[6,1,128,128]{3,2,1,0:T(8,128)S(1)} %pad.38, ...), kind=kLoop, calls=%fused_computation.61 | loop fusion | flops 56623104 | bytes 51249152 | tf_op jit(solution)/shard_map/add | solution.py:66
  64.2 4.4 %collective-permute-start.6 = (f32[1,32,128,128]{3,2,1,0:T(8,128)S(1)}, f32[1,32,128,128]{3,2,1,0:T(8,128)S(1)}, u32[]{:S(2)}, u32[]{:S(2)}) collective-permute-start(f32[1,32,128,128]{3,2,1,0:T(8,128)S(1)} %get-tuple-element.13), channel_id=1, source_target_pairs={{0,16},{16,32},{32,48},{48,64},{64,80},{80,96},{96,112},{1,17},{17... | collective-permute-start | bytes 6291464 | tf_op jit(solution)/shard_map/ppermute | solution.py:17
  71.6 3.1 %collective-permute-start.8 = (f32[4,1,128,128]{3,2,1,0:T(8,128)S(1)}, f32[4,1,128,128]{3,2,1,0:T(8,128)S(1)}, u32[]{:S(2)}, u32[]{:S(2)}) collective-permute-start(f32[4,1,128,128]{3,2,1,0:T(8,128)S(1)} %get-tuple-element.15), channel_id=1, source_target_pairs={{0,4},{4,8},{8,12},{1,5},{5,9},{9,13},{2,6},{6,10},{10,14},{3,7},{... | collective-permute-start | bytes 786440 | tf_op jit(solution)/shard_map/ppermute | solution.py:17
  77.4 3.2 %collective-permute-start.10 = (f32[4,32,1,128]{3,2,1,0:T(1,128)S(1)}, f32[4,32,1,128]{3,2,1,0:T(1,128)S(1)}, u32[]{:S(2)}, u32[]{:S(2)}) collective-permute-start(f32[4,32,1,128]{3,2,1,0:T(1,128)S(1)} %get-tuple-element.11), channel_id=1, source_target_pairs={{0,1},{1,2},{2,3},{4,5},{5,6},{6,7},{8,9},{9,10},{10,11},{12,13},{... | collective-permute-start | bytes 196616 | tf_op jit(solution)/shard_map/ppermute | solution.py:17
  83.0 2.6 %collective-permute-done.11 = f32[4,32,1,128]{3,2,1,0:T(1,128)S(1)} collective-permute-done((f32[4,32,1,128]{3,2,1,0:T(1,128)S(1)}, f32[4,32,1,128]{3,2,1,0:T(1,128)S(1)}, u32[]{:S(2)}, u32[]{:S(2)}) %collective-permute-start.11) | collective-permute-done | bytes 65568 | tf_op jit(solution)/shard_map/ppermute | solution.py:18
  85.6 6.0 %collective-permute-done.6 = f32[1,32,128,128]{3,2,1,0:T(8,128)S(1)} collective-permute-done((f32[1,32,128,128]{3,2,1,0:T(8,128)S(1)}, f32[1,32,128,128]{3,2,1,0:T(8,128)S(1)}, u32[]{:S(2)}, u32[]{:S(2)}) %collective-permute-start.6) | collective-permute-done | bytes 2097184 | tf_op jit(solution)/shard_map/ppermute | solution.py:17
  91.6 4.5 %collective-permute-done.7 = f32[1,32,128,128]{3,2,1,0:T(8,128)} collective-permute-done((f32[1,32,128,128]{3,2,1,0:T(8,128)S(1)}, f32[1,32,128,128]{3,2,1,0:T(8,128)}, u32[]{:S(2)}, u32[]{:S(2)}) %collective-permute-start.7) | collective-permute-done | bytes 2097184 | tf_op jit(solution)/shard_map/ppermute | solution.py:18
  96.1 28.4 %fusion.14 = f32[4,32,128,128]{3,2,1,0:T(8,128)} fusion(f32[4,32,128,128]{3,2,1,0:T(8,128)} %param.5, f32[4,32,1,128]{3,2,1,0:T(1,128)S(1)} %collective-permute-done.11, f32[6,1,128,128]{3,2,1,0:T(8,128)S(1)} %pad.43, f32[6,1,128,128]{3,2,1,0:T(8,128)S(1)} %pad.42, f32[1,32,128,128]{3,2,1,0:T(8,128)} %collective-permute-done.7, ...), kind=kLoop, calls=%fused_computation.33 | loop fusion | flops 73400320 | bytes 38666240 | tf_op jit(solution)/shard_map/add | solution.py:66
  128.9 2.5 %collective-permute-start.13 = (f32[1,32,128,128]{3,2,1,0:T(8,128)S(1)}, f32[1,32,128,128]{3,2,1,0:T(8,128)}, u32[]{:S(2)}, u32[]{:S(2)}) collective-permute-start(f32[1,32,128,128]{3,2,1,0:T(8,128)S(1)} %get-tuple-element.10), channel_id=1, source_target_pairs={{16,0},{32,16},{48,32},{64,48},{80,64},{96,80},{112,96},{17,1},{33... | collective-permute-start | bytes 6291464 | tf_op jit(solution)/shard_map/ppermute | solution.py:18
  132.5 3.1 %collective-permute-start.14 = (f32[4,1,128,128]{3,2,1,0:T(8,128)S(1)}, f32[4,1,128,128]{3,2,1,0:T(8,128)S(1)}, u32[]{:S(2)}, u32[]{:S(2)}) collective-permute-start(f32[4,1,128,128]{3,2,1,0:T(8,128)S(1)} %get-tuple-element.7), channel_id=1, source_target_pairs={{0,4},{4,8},{8,12},{1,5},{5,9},{9,13},{2,6},{6,10},{10,14},{3,7},{... | collective-permute-start | bytes 786440 | tf_op jit(solution)/shard_map/ppermute | solution.py:17
  138.3 3.2 %collective-permute-start.16 = (f32[4,32,1,128]{3,2,1,0:T(1,128)S(1)}, f32[4,32,1,128]{3,2,1,0:T(1,128)S(1)}, u32[]{:S(2)}, u32[]{:S(2)}) collective-permute-start(f32[4,32,1,128]{3,2,1,0:T(1,128)S(1)} %get-tuple-element.5), channel_id=1, source_target_pairs={{0,1},{1,2},{2,3},{4,5},{5,6},{6,7},{8,9},{9,10},{10,11},{12,13},{... | collective-permute-start | bytes 196616 | tf_op jit(solution)/shard_map/ppermute | solution.py:17
  143.2 2.6 %collective-permute-done.15 = f32[4,1,128,128]{3,2,1,0:T(8,128)S(1)} collective-permute-done((f32[4,1,128,128]{3,2,1,0:T(8,128)S(1)}, f32[4,1,128,128]{3,2,1,0:T(8,128)S(1)}, u32[]{:S(2)}, u32[]{:S(2)}) %collective-permute-start.15) | collective-permute-done | bytes 262176 | tf_op jit(solution)/shard_map/ppermute | solution.py:18
  147.0 4.8 %collective-permute-done.12 = f32[1,32,128,128]{3,2,1,0:T(8,128)S(1)} collective-permute-done((f32[1,32,128,128]{3,2,1,0:T(8,128)S(1)}, f32[1,32,128,128]{3,2,1,0:T(8,128)S(1)}, u32[]{:S(2)}, u32[]{:S(2)}) %collective-permute-start.12) | collective-permute-done | bytes 2097184 | tf_op jit(solution)/shard_map/ppermute | solution.py:17
  151.8 4.8 %collective-permute-done.13 = f32[1,32,128,128]{3,2,1,0:T(8,128)} collective-permute-done((f32[1,32,128,128]{3,2,1,0:T(8,128)S(1)}, f32[1,32,128,128]{3,2,1,0:T(8,128)}, u32[]{:S(2)}, u32[]{:S(2)}) %collective-permute-start.13) | collective-permute-done | bytes 2097184 | tf_op jit(solution)/shard_map/ppermute | solution.py:18
  156.6 28.8 %add_reduce_fusion = (f32[4,32,128]{2,1,0:T(8,128)S(1)}, f32[4,32,128]{2,1,0:T(8,128)S(1)}, f32[4,32,128,128]{3,2,1,0:T(8,128)}) fusion(f32[4,32,128,128]{3,2,1,0:T(8,128)} %param.5, f32[4,32,128,128]{3,2,1,0:T(8,128)} %fusion.14, f32[4,32,1,128]{3,2,1,0:T(1,128)S(1)} %collective-permute-done.17, f32[6,1,128,128]{3,2,1,0:T(8,128)S(1)} %pad.47, ...), kind=kLoop, calls=%fused_computation.80 | loop fusion | flops 81756160 | bytes 38797312 | tf_op jit(solution)/shard_map/reduce_sum | solution.py:78
  185.7 10.9 %all_to_all.6 = f32[4,1,32768]{2,1,0:T(1,128)S(1)} all-to-all(f32[4,1,32768]{2,1,0:T(1,128)S(1)} %broadcast_in_dim.2), channel_id=1, replica_groups=mesh['rows'=8,'cols'=4,'slabs'=4] {'slabs'}, dimensions={0} | all-to-all | bytes 1048576 | tf_op jit(solution)/shard_map/all_to_all | solution.py:31
  197.2 8.8 %subtract_multiply_fusion = f32[4,32,128,128]{3,2,1,0:T(8,128)} fusion(f32[4,32,128,128]{3,2,1,0:T(8,128)} %get-tuple-element.4, f32[4,32,128]{2,1,0:T(8,128)S(1)} %bitcast.7, f32[4,32,128]{2,1,0:T(8,128)S(1)} %bitcast.6), kind=kLoop, calls=%fused_computation.78 | loop fusion | flops 4194304 | bytes 16908288 | tf_op jit(solution)/shard_map/mul | solution.py:84
  (43 shorter events, 31.3 us)
Async XLA Ops:
  0.6 9.8 %copy-start = (f32[4,32,128,128]{3,2,1,0:T(8,128)S(1)}, f32[4,32,128,128]{3,2,1,0:T(8,128)}, u32[]{:S(2)}) copy-start(f32[4,32,128,128]{3,2,1,0:T(8,128)} %param.3) | copy-start | bytes 25165828
  3.3 28.2 %collective-permute-start = (f32[1,32,128,128]{3,2,1,0:T(8,128)S(1)}, f32[1,32,128,128]{3,2,1,0:T(8,128)S(1)}, u32[]{:S(2)}, u32[]{:S(2)}) collective-permute-start(f32[1,32,128,128]{3,2,1,0:T(8,128)S(1)} %get-tuple-element.22), channel_id=1, source_target_pairs={{0,16},{16,32},{32,48},{48,64},{64,80},{80,96},{96,112},{1,17},{17... | collective-permute-start | bytes 6291464 | tf_op jit(solution)/shard_map/ppermute | solution.py:17
  8.5 28.4 %collective-permute-start.1 = (f32[1,32,128,128]{3,2,1,0:T(8,128)S(1)}, f32[1,32,128,128]{3,2,1,0:T(8,128)S(1)}, u32[]{:S(2)}, u32[]{:S(2)}) collective-permute-start(f32[1,32,128,128]{3,2,1,0:T(8,128)S(1)} %get-tuple-element.21), channel_id=1, source_target_pairs={{16,0},{32,16},{48,32},{64,48},{80,64},{96,80},{112,96},{17,1},{33... | collective-permute-start | bytes 6291464 | tf_op jit(solution)/shard_map/ppermute | solution.py:18
  10.5 7.8 %collective-permute-start.2 = (f32[4,1,128,128]{3,2,1,0:T(8,128)S(1)}, f32[4,1,128,128]{3,2,1,0:T(8,128)S(1)}, u32[]{:S(2)}, u32[]{:S(2)}) collective-permute-start(f32[4,1,128,128]{3,2,1,0:T(8,128)S(1)} %get-tuple-element.19), channel_id=1, source_target_pairs={{0,4},{4,8},{8,12},{1,5},{5,9},{9,13},{2,6},{6,10},{10,14},{3,7},{... | collective-permute-start | bytes 786440 | tf_op jit(solution)/shard_map/ppermute | solution.py:17
  13.6 8.8 %collective-permute-start.3 = (f32[4,1,128,128]{3,2,1,0:T(8,128)S(1)}, f32[4,1,128,128]{3,2,1,0:T(8,128)S(1)}, u32[]{:S(2)}, u32[]{:S(2)}) collective-permute-start(f32[4,1,128,128]{3,2,1,0:T(8,128)S(1)} %get-tuple-element.20), channel_id=1, source_target_pairs={{4,0},{8,4},{12,8},{5,1},{9,5},{13,9},{6,2},{10,6},{14,10},{7,3},{... | collective-permute-start | bytes 786440 | tf_op jit(solution)/shard_map/ppermute | solution.py:18
  15.0 24.7 %collective-permute-start.4 = (f32[4,32,1,128]{3,2,1,0:T(1,128)S(1)}, f32[4,32,1,128]{3,2,1,0:T(1,128)S(1)}, u32[]{:S(2)}, u32[]{:S(2)}) collective-permute-start(f32[4,32,1,128]{3,2,1,0:T(1,128)S(1)} %get-tuple-element.17), channel_id=1, source_target_pairs={{0,1},{1,2},{2,3},{4,5},{5,6},{6,7},{8,9},{9,10},{10,11},{12,13},{... | collective-permute-start | bytes 196616 | tf_op jit(solution)/shard_map/ppermute | solution.py:17
  18.2 21.4 %collective-permute-start.5 = (f32[4,32,1,128]{3,2,1,0:T(1,128)S(1)}, f32[4,32,1,128]{3,2,1,0:T(1,128)S(1)}, u32[]{:S(2)}, u32[]{:S(2)}) collective-permute-start(f32[4,32,1,128]{3,2,1,0:T(1,128)S(1)} %get-tuple-element.18), channel_id=1, source_target_pairs={{1,0},{2,1},{3,2},{5,4},{6,5},{7,6},{9,8},{10,9},{11,10},{13,12},{... | collective-permute-start | bytes 196616 | tf_op jit(solution)/shard_map/ppermute | solution.py:18
  36.9 1.3 copy-start.1
  64.2 27.4 %collective-permute-start.6 = (f32[1,32,128,128]{3,2,1,0:T(8,128)S(1)}, f32[1,32,128,128]{3,2,1,0:T(8,128)S(1)}, u32[]{:S(2)}, u32[]{:S(2)}) collective-permute-start(f32[1,32,128,128]{3,2,1,0:T(8,128)S(1)} %get-tuple-element.13), channel_id=1, source_target_pairs={{0,16},{16,32},{32,48},{48,64},{64,80},{80,96},{96,112},{1,17},{17... | collective-permute-start | bytes 6291464 | tf_op jit(solution)/shard_map/ppermute | solution.py:17
  68.6 27.5 %collective-permute-start.7 = (f32[1,32,128,128]{3,2,1,0:T(8,128)S(1)}, f32[1,32,128,128]{3,2,1,0:T(8,128)}, u32[]{:S(2)}, u32[]{:S(2)}) collective-permute-start(f32[1,32,128,128]{3,2,1,0:T(8,128)S(1)} %get-tuple-element.14), channel_id=1, source_target_pairs={{16,0},{32,16},{48,32},{64,48},{80,64},{96,80},{112,96},{17,1},{33... | collective-permute-start | bytes 6291464 | tf_op jit(solution)/shard_map/ppermute | solution.py:18
  71.6 9.0 %collective-permute-start.8 = (f32[4,1,128,128]{3,2,1,0:T(8,128)S(1)}, f32[4,1,128,128]{3,2,1,0:T(8,128)S(1)}, u32[]{:S(2)}, u32[]{:S(2)}) collective-permute-start(f32[4,1,128,128]{3,2,1,0:T(8,128)S(1)} %get-tuple-element.15), channel_id=1, source_target_pairs={{0,4},{4,8},{8,12},{1,5},{5,9},{9,13},{2,6},{6,10},{10,14},{3,7},{... | collective-permute-start | bytes 786440 | tf_op jit(solution)/shard_map/ppermute | solution.py:17
  74.8 8.2 %collective-permute-start.9 = (f32[4,1,128,128]{3,2,1,0:T(8,128)S(1)}, f32[4,1,128,128]{3,2,1,0:T(8,128)S(1)}, u32[]{:S(2)}, u32[]{:S(2)}) collective-permute-start(f32[4,1,128,128]{3,2,1,0:T(8,128)S(1)} %get-tuple-element.16), channel_id=1, source_target_pairs={{4,0},{8,4},{12,8},{5,1},{9,5},{13,9},{6,2},{10,6},{14,10},{7,3},{... | collective-permute-start | bytes 786440 | tf_op jit(solution)/shard_map/ppermute | solution.py:18
  77.4 5.6 %collective-permute-start.10 = (f32[4,32,1,128]{3,2,1,0:T(1,128)S(1)}, f32[4,32,1,128]{3,2,1,0:T(1,128)S(1)}, u32[]{:S(2)}, u32[]{:S(2)}) collective-permute-start(f32[4,32,1,128]{3,2,1,0:T(1,128)S(1)} %get-tuple-element.11), channel_id=1, source_target_pairs={{0,1},{1,2},{2,3},{4,5},{5,6},{6,7},{8,9},{9,10},{10,11},{12,13},{... | collective-permute-start | bytes 196616 | tf_op jit(solution)/shard_map/ppermute | solution.py:17
  80.6 5.0 %collective-permute-start.11 = (f32[4,32,1,128]{3,2,1,0:T(1,128)S(1)}, f32[4,32,1,128]{3,2,1,0:T(1,128)S(1)}, u32[]{:S(2)}, u32[]{:S(2)}) collective-permute-start(f32[4,32,1,128]{3,2,1,0:T(1,128)S(1)} %get-tuple-element.12), channel_id=1, source_target_pairs={{1,0},{2,1},{3,2},{5,4},{6,5},{7,6},{9,8},{10,9},{11,10},{13,12},{... | collective-permute-start | bytes 196616 | tf_op jit(solution)/shard_map/ppermute | solution.py:18
  127.0 24.9 %collective-permute-start.12 = (f32[1,32,128,128]{3,2,1,0:T(8,128)S(1)}, f32[1,32,128,128]{3,2,1,0:T(8,128)S(1)}, u32[]{:S(2)}, u32[]{:S(2)}) collective-permute-start(f32[1,32,128,128]{3,2,1,0:T(8,128)S(1)} %get-tuple-element.9), channel_id=1, source_target_pairs={{0,16},{16,32},{32,48},{48,64},{64,80},{80,96},{96,112},{1,17},{17... | collective-permute-start | bytes 6291464 | tf_op jit(solution)/shard_map/ppermute | solution.py:17
  128.9 27.7 %collective-permute-start.13 = (f32[1,32,128,128]{3,2,1,0:T(8,128)S(1)}, f32[1,32,128,128]{3,2,1,0:T(8,128)}, u32[]{:S(2)}, u32[]{:S(2)}) collective-permute-start(f32[1,32,128,128]{3,2,1,0:T(8,128)S(1)} %get-tuple-element.10), channel_id=1, source_target_pairs={{16,0},{32,16},{48,32},{64,48},{80,64},{96,80},{112,96},{17,1},{33... | collective-permute-start | bytes 6291464 | tf_op jit(solution)/shard_map/ppermute | solution.py:18
  132.5 9.1 %collective-permute-start.14 = (f32[4,1,128,128]{3,2,1,0:T(8,128)S(1)}, f32[4,1,128,128]{3,2,1,0:T(8,128)S(1)}, u32[]{:S(2)}, u32[]{:S(2)}) collective-permute-start(f32[4,1,128,128]{3,2,1,0:T(8,128)S(1)} %get-tuple-element.7), channel_id=1, source_target_pairs={{0,4},{4,8},{8,12},{1,5},{5,9},{9,13},{2,6},{6,10},{10,14},{3,7},{... | collective-permute-start | bytes 786440 | tf_op jit(solution)/shard_map/ppermute | solution.py:17
  135.6 10.1 %collective-permute-start.15 = (f32[4,1,128,128]{3,2,1,0:T(8,128)S(1)}, f32[4,1,128,128]{3,2,1,0:T(8,128)S(1)}, u32[]{:S(2)}, u32[]{:S(2)}) collective-permute-start(f32[4,1,128,128]{3,2,1,0:T(8,128)S(1)} %get-tuple-element.8), channel_id=1, source_target_pairs={{4,0},{8,4},{12,8},{5,1},{9,5},{13,9},{6,2},{10,6},{14,10},{7,3},{... | collective-permute-start | bytes 786440 | tf_op jit(solution)/shard_map/ppermute | solution.py:18
  138.3 7.5 %collective-permute-start.16 = (f32[4,32,1,128]{3,2,1,0:T(1,128)S(1)}, f32[4,32,1,128]{3,2,1,0:T(1,128)S(1)}, u32[]{:S(2)}, u32[]{:S(2)}) collective-permute-start(f32[4,32,1,128]{3,2,1,0:T(1,128)S(1)} %get-tuple-element.5), channel_id=1, source_target_pairs={{0,1},{1,2},{2,3},{4,5},{5,6},{6,7},{8,9},{9,10},{10,11},{12,13},{... | collective-permute-start | bytes 196616 | tf_op jit(solution)/shard_map/ppermute | solution.py:17
  141.7 5.4 %collective-permute-start.17 = (f32[4,32,1,128]{3,2,1,0:T(1,128)S(1)}, f32[4,32,1,128]{3,2,1,0:T(1,128)S(1)}, u32[]{:S(2)}, u32[]{:S(2)}) collective-permute-start(f32[4,32,1,128]{3,2,1,0:T(1,128)S(1)} %get-tuple-element.6), channel_id=1, source_target_pairs={{1,0},{2,1},{3,2},{5,4},{6,5},{7,6},{9,8},{10,9},{11,10},{13,12},{... | collective-permute-start | bytes 196616 | tf_op jit(solution)/shard_map/ppermute | solution.py:18
where the time goes:
time: 208 us; the launch traced here: 206 us
  other arithmetic  88.6 us (43%)
  starting transfers between devices  44.8 us (22%)
  waiting for transfers between devices  39.6 us (19%)
  local copies, waits for them, and re-layouts  21.2 us (10%)
  blocking collectives  10.9 us (5%)
    add x2, other arithmetic, march_step(): return 2.0 * middle - before + speed_square * spread  50.4 us
    ppermute x9, starting transfers between devices, extended(): lax.ppermute(last, axis, up)  30.5 us
    reduce_sum x1, other arithmetic, shards(): jnp.sum(moved, axis=2, keepdims=True)  28.8 us
    ppermute x9, waiting for transfers between devices, extended(): lax.ppermute(last, axis, up)  20 us
    ppermute x9, waiting for transfers between devices, extended(): lax.ppermute(leading, axis, [(b, a) for a, b in up])  19.6 us
    ppermute x9, starting transfers between devices, extended(): lax.ppermute(leading, axis, [(b, a) for a, b in up])  14.3 us
    all_to_all x1, blocking collectives, sent_to_all(): lax.all_to_all(jnp.broadcast_to(value[None], (length, *value.shape)), axi...  10.9 us
    slice x8, local copies, waits for them, and re-layouts, extended(): last = lax.slice_in_dim(value, length - width, length, axis=dim)  9.87 us
  transfers between devices with their start and end apart: 18, of which 11 were waited for; matrix products, arithmetic and copies ran while one was open for 6% of the time, Pallas kernels for 0%

commit v1 on v0

v1 whole, which is shorter than its diff:
```python
import functools

import jax
import jax.numpy as jnp
from jax import lax
from jax.experimental import pallas as pl
from jax.experimental.pallas import tpu as pltpu
from jax.sharding import PartitionSpec as P

STEPS = 3
R = 4
PAD = 8
MESH = pl.DeviceIdType.MESH
F32 = jnp.float32


def march_kernel(
    shape, sizes, now_hbm, before_hbm, speed_hbm,
    last, mean_out, scale_out,
    even, odd, speed, stats,
    load_sem, z_send, z_recv, x_send, x_recv, y_send, y_recv, s_send, s_recv,
):
    J, I, K, M = shape
    rows, cols, slabs = sizes
    N = I // R
    LINES = J * R
    row, col, slab = (lax.axis_index(a) for a in ("rows", "cols", "slabs"))
    has = {
        "rows": (row > 0, row < rows - 1),
        "cols": (col > 0, col < cols - 1),
        "slabs": (slab > 0, slab < slabs - 1),
    }
    beside = {
        "rows": (row - 1, row + 1),
        "cols": (col - 1, col + 1),
        "slabs": (slab - 1, slab + 1),
    }
    jj, kk = pl.ds(1, J), pl.ds(PAD, K)
    fields = (even, odd, even)

    def span(c):
        return pl.ds(c * R, R)

    def inner(c):
        return pl.ds(1 + c * R, R)

    def z_copy(s, side, c):
        f = fields[s]
        edge = 0 if side == 0 else J - 1
        src = now_hbm.at[edge, span(c)] if s == 0 else f.at[1 + edge, inner(c), kk]
        dst = f.at[J + 1 if side == 0 else 0, inner(c), kk]
        return pltpu.make_async_remote_copy(
            src, dst, z_send.at[s, side, c], z_recv.at[s, side, c],
            device_id={"rows": beside["rows"][side]}, device_id_type=MESH)

    def x_copy(s, side):
        f = fields[s]
        edge = 0 if side == 0 else I - 1
        src = now_hbm.at[:, edge] if s == 0 else f.at[jj, 1 + edge, kk]
        dst = f.at[jj, I + 1 if side == 0 else 0, kk]
        return pltpu.make_async_remote_copy(
            src, dst, x_send.at[s, side], x_recv.at[s, side],
            device_id={"cols": beside["cols"][side]}, device_id_type=MESH)

    def y_copy(s, side, c):
        f = fields[s]
        edge = 0 if side == 0 else K - PAD
        if s == 0:
            src = now_hbm.at[:, span(c), pl.ds(edge, PAD)]
        else:
            src = f.at[jj, inner(c), pl.ds(PAD + edge, PAD)]
        dst = f.at[jj, inner(c), pl.ds(PAD + K if side == 0 else 0, PAD)]
        return pltpu.make_async_remote_copy(
            src, dst, y_send.at[s, side, c], y_recv.at[s, side, c],
            device_id={"slabs": beside["slabs"][side]}, device_id_type=MESH)

    def s_copy(d, c):
        part = stats.at[slab, c]
        return pltpu.make_async_remote_copy(
            part, part, s_send.at[d - 1, c], s_recv.at[d - 1, c],
            device_id={"slabs": lax.rem(slab + d, slabs)}, device_id_type=MESH)

    def load(k, c):
        src, dst = (
            (now_hbm, even.at[jj, inner(c), kk]),
            (before_hbm, odd.at[jj, inner(c), kk]),
            (speed_hbm, speed.at[:, span(c)]),
        )[k]
        return pltpu.make_async_copy(src.at[:, span(c)], dst, load_sem.at[k, c])

    barrier = pltpu.get_barrier_semaphore()
    count = jnp.int32(slabs - 1)
    for axis in ("rows", "cols"):
        for side in (0, 1):
            there = has[axis][side]
            count = count + there.astype(jnp.int32)

            @pl.when(there)
            def _():
                pl.semaphore_signal(barrier, inc=1, device_id={axis: beside[axis][side]}, device_id_type=MESH)
    for d in range(1, slabs):
        pl.semaphore_signal(barrier, inc=1, device_id={"slabs": lax.rem(slab + d, slabs)}, device_id_type=MESH)

    @pl.loop(0, N)
    def _(c):
        for k in range(3):
            load(k, c).start()

    for f in (even, odd):
        for side, (z, x, y) in enumerate(((0, 0, 0), (J + 1, I + 1, PAD + K))):
            @pl.when(jnp.logical_not(has["rows"][side]))
            def _():
                @pl.loop(0, I)
                def _(i):
                    f[z, 1 + i, kk] = jnp.zeros((K, M), F32)

            @pl.when(jnp.logical_not(has["cols"][side]))
            def _():
                @pl.loop(0, J)
                def _(j):
                    f[1 + j, x, kk] = jnp.zeros((K, M), F32)

            @pl.when(jnp.logical_not(has["slabs"][side]))
            def _():
                @pl.loop(0, I)
                def _(i):
                    for j in range(J):
                        f[1 + j, 1 + i, pl.ds(y, PAD)] = jnp.zeros((PAD, M), F32)

    pl.semaphore_wait(barrier, count)

    def for_sides(axis, act):
        for side in (0, 1):
            @pl.when(has[axis][side])
            def _():
                act(side)

    @pl.loop(0, N)
    def _(c):
        for_sides("rows", lambda side: z_copy(0, side, c).start())
        for_sides("slabs", lambda side: y_copy(0, side, c).start())

    for_sides("cols", lambda side: x_copy(0, side).start())

    def line(s, j, i):
        f, g = fields[s], fields[(s + 1) % 2]
        centre = f[1 + j, 1 + i, kk]
        total = f[j, 1 + i, kk] + f[j + 2, 1 + i, kk]
        total = total + (f[1 + j, i, kk] + f[1 + j, i + 2, kk])
        total = total + (f[1 + j, 1 + i, pl.ds(PAD - 1, K)] + f[1 + j, 1 + i, pl.ds(PAD + 1, K)])
        old = g[1 + j, 1 + i, kk]
        return (2.0 * centre - old) + speed[j, i] * (total - 6.0 * centre)

    def step_lines(s, c, planes):
        first, stride = planes

        @pl.loop(0, 2)
        def _(p):
            j = first + stride * p
            if s < STEPS - 1:
                @pl.loop(0, R)
                def _(r):
                    i = c * R + r
                    fields[(s + 1) % 2][1 + j, 1 + i, kk] = line(s, j, i)
            else:
                @pl.loop(0, R)
                def _(r):
                    i = c * R + r
                    value = line(s, j, i)
                    last[j, i] = value
                    mean = jnp.sum(value, axis=0, keepdims=True) * (1.0 / K)
                    away = value - mean
                    at = pl.ds(j * R + r, 1)
                    stats[slab, c, 0, at, :] = mean
                    stats[slab, c, 1, at, :] = jnp.sum(away * away, axis=0, keepdims=True)

    def finish(c):
        for d in range(1, slabs):
            s_copy(d, c).wait_recv()
        means = [stats[b, c, 0] for b in range(slabs)]
        mean = sum(means[1:], means[0]) * (1.0 / slabs)
        spread = sum((stats[b, c, 1] for b in range(1, slabs)), stats[0, c, 1])
        apart = sum(((m - mean) * (m - mean) for m in means[1:]), (means[0] - mean) * (means[0] - mean))
        variance = (spread + K * apart) * (1.0 / (K * slabs))
        mean_out[c] = mean
        scale_out[c] = lax.rsqrt(variance + 0.0001)

    def wait_sides(axis, copy):
        for side in (0, 1):
            @pl.when(has[axis][1 - side])
            def _():
                copy(side).wait_recv()

    for s in range(STEPS):
        if s == 0:
            load(0, 0).wait()

        @pl.loop(0, N)
        def _(c):
            if s == 0:
                @pl.when(c + 1 < N)
                def _():
                    load(0, c + 1).wait()

                for k in (1, 2):
                    load(k, c).wait()
            wait_sides("slabs", lambda side: y_copy(s, side, c))

            @pl.when(jnp.logical_and(c == 0, has["cols"][0]))
            def _():
                x_copy(s, 1).wait_recv()

            @pl.when(jnp.logical_and(c == N - 1, has["cols"][1]))
            def _():
                x_copy(s, 0).wait_recv()

            if s < STEPS - 1:
                wait_sides("rows", lambda side: z_copy(s, side, c))
                step_lines(s, c, (0, J - 1))
                step_lines(s, c, (1, 1))
                for_sides("rows", lambda side: z_copy(s + 1, side, c).start())
                for_sides("slabs", lambda side: y_copy(s + 1, side, c).start())

                @pl.when(jnp.logical_and(c == 0, has["cols"][0]))
                def _():
                    x_copy(s + 1, 0).start()

                @pl.when(jnp.logical_and(c == N - 1, has["cols"][1]))
                def _():
                    x_copy(s + 1, 1).start()
            else:
                step_lines(s, c, (1, 1))
                wait_sides("rows", lambda side: z_copy(s, side, c))
                step_lines(s, c, (0, J - 1))
                for d in range(1, slabs):
                    s_copy(d, c).start()

                @pl.when(c > 0)
                def _():
                    finish(c - 1)

    for s in range(STEPS):
        @pl.loop(0, N)
        def _(c):
            for_sides("rows", lambda side: z_copy(s, side, c).wait_send())
            for_sides("slabs", lambda side: y_copy(s, side, c).wait_send())

        for_sides("cols", lambda side: x_copy(s, side).wait_send())

    finish(N - 1)

    @pl.loop(0, N)
    def _(c):
        for d in range(1, slabs):
            s_copy(d, c).wait_send()


def write_kernel(shape, last, mean, scale, scaled_hbm, end_hbm, scaled, sems):
    J, I, K, M = shape
    N = I // R

    def end_copy(c):
        span = pl.ds(c * R, R)
        return pltpu.make_async_copy(last.at[:, span], end_hbm.at[:, span], sems.at[0, c])

    def scaled_copy(c):
        span = pl.ds(c * R, R)
        return pltpu.make_async_copy(scaled.at[:, span], scaled_hbm.at[:, span], sems.at[1, c])

    @pl.loop(0, N)
    def _(c):
        end_copy(c).start()

    @pl.loop(0, N)
    def _(c):
        @pl.loop(0, J)
        def _(j):
            for r in range(R):
                at = pl.ds(j * R + r, 1)
                i = c * R + r
                scaled[j, i] = (last[j, i] - mean[c, at, :]) * scale[c, at, :]
        scaled_copy(c).start()

    @pl.loop(0, N)
    def _(c):
        end_copy(c).wait()
        scaled_copy(c).wait()


def shards(sizes, field_now, earlier, speed_square):
    shape = field_now.shape
    J, I, K, M = shape
    N = I // R
    slabs = sizes[2]
    hbm = pl.BlockSpec(memory_space=pltpu.HBM)
    vmem = pl.BlockSpec(memory_space=pltpu.VMEM)
    dma = pltpu.SemaphoreType.DMA
    padded = pltpu.VMEM((J + 2, I + 2, K + 2 * PAD, M), F32)
    last, mean, scale = pl.pallas_call(
        functools.partial(march_kernel, shape, sizes),
        out_shape=(
            pltpu.VMEM(shape, F32),
            pltpu.VMEM((N, J * R, M), F32),
            pltpu.VMEM((N, J * R, M), F32),
        ),
        in_specs=[hbm, hbm, hbm],
        out_specs=(vmem, vmem, vmem),
        scratch_shapes=[
            padded,
            padded,
            pltpu.VMEM(shape, F32),
            pltpu.VMEM((slabs, N, 2, J * R, M), F32),
            dma((3, N)),
            dma((STEPS, 2, N)),
            dma((STEPS, 2, N)),
            dma((STEPS, 2)),
            dma((STEPS, 2)),
            dma((STEPS, 2, N)),
            dma((STEPS, 2, N)),
            dma((slabs - 1, N)),
            dma((slabs - 1, N)),
        ],
        compiler_params=pltpu.CompilerParams(
            collective_id=0, has_side_effects=True, vmem_limit_bytes=44 * 2**20
        ),
        name="march",
    )(field_now, earlier, speed_square)
    return pl.pallas_call(
        functools.partial(write_kernel, shape),
        out_shape=(jax.ShapeDtypeStruct(shape, F32), jax.ShapeDtypeStruct(shape, F32)),
        in_specs=[vmem, vmem, vmem],
        out_specs=(hbm, hbm),
        scratch_shapes=[pltpu.VMEM(shape, F32), dma((2, N))],
        compiler_params=pltpu.CompilerParams(vmem_limit_bytes=12 * 2**20),
        name="write",
    )(last, mean, scale)


def solution(mesh):
    placed = P("rows", "cols", "slabs", None)
    sizes = tuple(mesh.shape[a] for a in ("rows", "cols", "slabs"))
    return jax.shard_map(
        functools.partial(shards, sizes),
        mesh=mesh,
        in_specs=(placed, placed, placed),
        out_specs=(placed, placed),
        check_vma=False,
    )
```

time: 208 us -> 87.5 us (0.42)
  other arithmetic: 88.6 us -> 0 us
  Pallas kernels: 0 us -> 86.7 us
  starting transfers between devices: 44.8 us -> 0 us
  waiting for transfers between devices: 39.6 us -> 0 us
  local copies, waits for them, and re-layouts: 21.2 us -> 0 us
  blocking collectives: 10.9 us -> 0 us
    pallas_call x0 -> x2, Pallas kernels: none -> 86.7 us  [the longest x1 80.8 us: shards(): pl.pallas_call(functools.partial(march_kernel, shape, sizes), out_shape=(...]
    add x3 -> x0, other arithmetic: 50.5 us -> none  [the longest x2 50.4 us: march_step(): return 2.0 * middle - before + speed_square * spread]
    ppermute x18 -> x0, starting transfers between devices: 44.8 us -> none  [the longest x9 30.5 us: extended(): lax.ppermute(last, axis, up)]
    ppermute x18 -> x0, waiting for transfers between devices: 39.6 us -> none  [the longest x9 20 us: extended(): lax.ppermute(last, axis, up)]
    reduce_sum x2 -> x0, other arithmetic: 29.3 us -> none  [the longest x1 28.8 us: shards(): jnp.sum(moved, axis=2, keepdims=True)]
    slice x9 -> x0, local copies, waits for them, and re-layouts: 12.5 us -> none  [the longest x8 9.87 us: extended(): last = lax.slice_in_dim(value, length - width, length, axis=dim)]
    all_to_all x1 -> x0, blocking collectives: 10.9 us -> none  [sent_to_all(): lax.all_to_all(jnp.broadcast_to(value[None], (length, *value.shape)), axi...]
    mul x1 -> x0, other arithmetic: 8.85 us -> none  [shards(): scaled_field = centred * lax.rsqrt(line_variance + 0.0001)]
  transfers between devices with their start and end apart: 18 -> 0, of which waited for: 11 -> 0; matrix products, arithmetic and copies ran while one was open for 6% -> 0% of each run, Pallas kernels for 0% -> 0%
where the time goes in v1:
time: 87.5 us; the launch traced here: 87.4 us
  Pallas kernels  86.7 us (99%)
    pallas_call x1, Pallas kernels, shards(): pl.pallas_call(functools.partial(march_kernel, shape, sizes), out_shape=(...  80.8 us
    pallas_call x1, Pallas kernels, shards(): pl.pallas_call(functools.partial(write_kernel, shape), out_shape=(jax.Sha...  5.96 us

profile of v1, /device:TPU:1, one launch (start us, length us, event | category | flops | bytes accessed | tf_op | source)
XLA Modules:
  0.0 87.4 jit_solution(4073658501893124099)
XLA Ops:
  0.6 80.8 %march.1 = (f32[4,32,128,128]{3,2,1,0:T(8,128)S(1)}, f32[8,16,128]{2,1,0:T(8,128)S(1)}, f32[8,16,128]{2,1,0:T(8,128)S(1)}) custom-call(f32[4,32,128,128]{3,2,1,0:T(8,128)} %now_hbm.1, f32[4,32,128,128]{3,2,1,0:T(8,128)} %before_hbm.1, f32[4,32,128,128]{3,2,1,0:T(8,128)} %speed_hbm.1), custom_call_target="tpu_custom_call" | custom-call | tf_op jit(solution)/shard_map/march/pallas_call | solution.py:299
  81.4 6.0 %write.1 = (f32[4,32,128,128]{3,2,1,0:T(8,128)}, f32[4,32,128,128]{3,2,1,0:T(8,128)}) custom-call(f32[4,32,128,128]{3,2,1,0:T(8,128)S(1)} %get-tuple-element.5.last, f32[8,16,128]{2,1,0:T(8,128)S(1)} %get-tuple-element.6.mean, f32[8,16,128]{2,1,0:T(8,128)S(1)} %get-tuple-element.7.scale), custom_call_target="tpu_custom_call" | custom-call | tf_op jit(solution)/shard_map/write/pallas_call | solution.py:328

commit v2 on v0

v2 whole, which is shorter than its diff:
```python
import functools

import jax
import jax.numpy as jnp
from jax import lax
from jax.experimental import pallas as pl
from jax.experimental.pallas import tpu as pltpu
from jax.sharding import PartitionSpec as P

STEPS = 3
PAD = 8
MESH = pl.DeviceIdType.MESH
F32 = jnp.float32


def chunks_of(rows, step):
    size = max(rows // 4, 2)
    cut = [(a, size) for a in range(0, rows, size)]
    if step == STEPS - 1:
        first, size = cut.pop()
        cut += [(first, size // 2), (first + size // 2, size // 2)]
    return cut


def march_kernel(
    shape, sizes, now_hbm, before_hbm, speed_hbm,
    last, lines_out,
    even, odd, speed, stats,
    load_sem, z_send, z_recv, x_send, x_recv, y_send, y_recv, s_send, s_recv,
    passed_on, further,
):
    J, I, K, M = shape
    rows, cols, slabs = sizes
    row, col, slab = (lax.axis_index(a) for a in ("rows", "cols", "slabs"))
    has = {
        "rows": (row > 0, row < rows - 1),
        "cols": (col > 0, col < cols - 1),
        "slabs": (slab > 0, slab < slabs - 1),
    }
    beside = {
        "rows": (row - 1, row + 1),
        "cols": (col - 1, col + 1),
        "slabs": (slab - 1, slab + 1),
    }
    upper_core = lax.rem(row, 2) == 1
    jj, ii, kk = pl.ds(1, J), pl.ds(1, I), pl.ds(PAD, K)
    fields = (even, odd, even)
    chunks = [chunks_of(I, s) for s in range(STEPS)]
    slot = [{cut: n for n, cut in enumerate(chunks[s])} for s in range(STEPS)]
    base = [(s % 2) * len(chunks[-1]) for s in range(STEPS)]

    def z_copy(s, side, cut):
        f = fields[s]
        a, n = cut
        edge = 0 if side == 0 else J - 1
        src = now_hbm.at[edge, pl.ds(a, n)] if s == 0 else f.at[1 + edge, pl.ds(1 + a, n), kk]
        dst = f.at[J + 1 if side == 0 else 0, pl.ds(1 + a, n), kk]
        return pltpu.make_async_remote_copy(
            src, dst, z_send.at[side], z_recv.at[side, base[s] + slot[s][cut]],
            device_id={"rows": beside["rows"][side]}, device_id_type=MESH)

    def x_copy(s, side):
        f = fields[s]
        edge = 0 if side == 0 else I - 1
        src = now_hbm.at[:, edge] if s == 0 else f.at[jj, 1 + edge, kk]
        dst = f.at[jj, I + 1 if side == 0 else 0, kk]
        return pltpu.make_async_remote_copy(
            src, dst, x_send.at[side], x_recv.at[s % 2, side],
            device_id={"cols": beside["cols"][side]}, device_id_type=MESH)

    def y_copy(s, side):
        f = fields[s]
        edge = 0 if side == 0 else K - 1
        src = now_hbm.at[:, :, pl.ds(edge, 1)] if s == 0 else f.at[jj, ii, pl.ds(PAD + edge, 1)]
        dst = f.at[jj, ii, pl.ds(PAD + K if side == 0 else PAD - 1, 1)]
        return pltpu.make_async_remote_copy(
            src, dst, y_send.at[side], y_recv.at[s % 2, side],
            device_id={"slabs": beside["slabs"][side]}, device_id_type=MESH)

    far = jnp.where(upper_core, J - 1, 0)
    early, late = 0, 1

    def s_copy(part, d, planes, cut):
        ref = stats.at[slab, :, planes, pl.ds(*cut)]
        return pltpu.make_async_remote_copy(
            ref, ref, s_send, s_recv.at[part, d - 1],
            device_id={"slabs": lax.rem(slab + d, slabs)}, device_id_type=MESH)

    def send_sums(part, planes, cut):
        for d in range(1, slabs):
            s_copy(part, d, planes, cut).start()

    def load(ref, buffer, c, sem):
        a, n = chunks[0][c]
        start = 1 if buffer is not speed else 0
        planes = jj if buffer is not speed else pl.ds(0, J)
        width = kk if buffer is not speed else pl.ds(0, K)
        return pltpu.make_async_copy(
            ref.at[:, pl.ds(a, n)], buffer.at[planes, pl.ds(start + a, n), width], load_sem.at[sem])

    def start_loads(c):
        if c + 1 < len(chunks[0]):
            load(now_hbm, even, c + 1, c + 1).start()
        if c < len(chunks[0]):
            load(before_hbm, odd, c, c + 1).start()
            load(speed_hbm, speed, c, c + 1).start()

    def wait_loads(c):
        a, n = chunks[0][c]
        amount = pl.ds(0, 3 * n if c + 1 < len(chunks[0]) else 2 * n)
        pltpu.make_async_copy(speed_hbm.at[:, amount], speed.at[:, amount], load_sem.at[c + 1]).wait()

    def for_sides(axis, act):
        for side in (0, 1):
            @pl.when(has[axis][side])
            def _():
                act(side)

    def wait_sides(axis, copy):
        for side in (0, 1):
            @pl.when(has[axis][1 - side])
            def _():
                copy(side).wait_recv()

    lower_core = jnp.logical_not(upper_core)
    around = [(axis, side) for axis in ("cols", "slabs") for side in (0, 1)]

    def number(places):
        return sum((has[axis][side].astype(jnp.int32) for axis, side in places), jnp.int32(0))

    def greet(sem, axis, side, when):
        @pl.when(jnp.logical_and(has[axis][side], when))
        def _():
            pl.semaphore_signal(sem, inc=1, device_id={axis: beside[axis][side]}, device_id_type=MESH)

    barrier = pltpu.get_barrier_semaphore()
    for side in (0, 1):
        greet(barrier, "rows", side, True)
    for axis, side in around:
        greet(barrier, axis, side, upper_core)
    load(now_hbm, even, 0, 0).start()
    start_loads(0)
    pl.semaphore_wait(barrier, number([("rows", 0), ("rows", 1)]) + jnp.where(upper_core, number(around), 0))
    for cut in chunks[0]:
        for_sides("rows", lambda side: z_copy(0, side, cut).start())
    for axis, side in around:
        greet(passed_on, axis, side, upper_core)
    pl.semaphore_wait(passed_on, jnp.where(upper_core, number(around), 1))

    @pl.when(upper_core)
    def _():
        pl.semaphore_signal(passed_on, inc=1, device_id={"rows": row - 1}, device_id_type=MESH)

    for_sides("slabs", lambda side: y_copy(0, side).start())
    for_sides("cols", lambda side: x_copy(0, side).start())
    start_loads(1)

    def tell(t):
        for side in (0, 1):
            greet(further.at[t], "slabs", side, True)

    def hear(t):
        pl.semaphore_wait(further.at[t], number([("slabs", 0), ("slabs", 1)]))

    tell(0)

    for f in (even, odd):
        for side, (z, x, y) in enumerate(((0, 0, PAD - 1), (J + 1, I + 1, PAD + K))):
            @pl.when(jnp.logical_not(has["rows"][side]))
            def _():
                @pl.loop(0, I)
                def _(i):
                    f[z, 1 + i, kk] = jnp.zeros((K, M), F32)

            @pl.when(jnp.logical_not(has["cols"][side]))
            def _():
                @pl.loop(0, J)
                def _(j):
                    f[1 + j, x, kk] = jnp.zeros((K, M), F32)

            @pl.when(jnp.logical_not(has["slabs"][side]))
            def _():
                @pl.loop(0, I)
                def _(i):
                    for j in range(J):
                        f[1 + j, 1 + i, pl.ds(y, 1)] = jnp.zeros((1, M), F32)

    def line(s, j, i):
        f, g = fields[s], fields[(s + 1) % 2]
        centre = f[1 + j, 1 + i, kk]
        total = f[j, 1 + i, kk] + f[j + 2, 1 + i, kk]
        total = total + (f[1 + j, i, kk] + f[1 + j, i + 2, kk])
        total = total + (f[1 + j, 1 + i, pl.ds(PAD - 1, K)] + f[1 + j, 1 + i, pl.ds(PAD + 1, K)])
        old = g[1 + j, 1 + i, kk]
        return (2.0 * centre - old) + speed[j, i] * (total - 6.0 * centre)

    def step_plane(s, cut, j):
        a, n = cut

        @pl.loop(a, a + n)
        def _(i):
            value = line(s, j, i)
            if s < STEPS - 1:
                fields[(s + 1) % 2][1 + j, 1 + i, kk] = value
            else:
                last[j, i] = value
                mean = jnp.sum(value, axis=0, keepdims=True) * (1.0 / K)
                away = value - mean
                stats[slab, 0, j, pl.ds(i, 1)] = mean
                stats[slab, 1, j, pl.ds(i, 1)] = jnp.sum(away * away, axis=0, keepdims=True)

    def step_inside(s, cut):
        @pl.loop(1, J - 1)
        def _(j):
            step_plane(s, cut, j)

    def wait_below(s, cut, when):
        @pl.when(jnp.logical_and(has["rows"][0], when))
        def _():
            z_copy(s, 1, cut).wait_recv()

    def wait_above(s, cut, when):
        @pl.when(jnp.logical_and(has["rows"][1], when))
        def _():
            z_copy(s, 0, cut).wait_recv()

    def step_outside(s, cut, between=None):
        wait_below(s, cut, upper_core)
        wait_above(s, cut, lower_core)
        step_plane(s, cut, J - 1 - far)
        if between is not None:
            between()
        wait_below(s, cut, lower_core)
        wait_above(s, cut, upper_core)
        step_plane(s, cut, far)

    def finish(planes, rows_i):
        @pl.loop(*planes)
        def _(j):
            at = pl.ds(*rows_i)
            means = [stats[b, 0, j, at] for b in range(slabs)]
            mean = sum(means[1:], means[0]) * (1.0 / slabs)
            spread = sum((stats[b, 1, j, at] for b in range(1, slabs)), stats[0, 1, j, at])
            apart = sum(((m - mean) * (m - mean) for m in means[1:]), (means[0] - mean) * (means[0] - mean))
            variance = (spread + K * apart) * (1.0 / (K * slabs))
            lines_out[0, j, at] = mean
            lines_out[1, j, at] = lax.rsqrt(variance + 0.0001)

    load(now_hbm, even, 0, 0).wait()
    for s in range(STEPS):
        for c, cut in enumerate(chunks[s]):
            a, n = cut
            if s == 0:
                start_loads(c + 2)
                wait_loads(c)
            if c == 0:
                wait_sides("slabs", lambda side: y_copy(s, side))

                @pl.when(has["cols"][0])
                def _():
                    x_copy(s, 1).wait_recv()
            if a + n == I:
                @pl.when(has["cols"][1])
                def _():
                    x_copy(s, 0).wait_recv()
            if s == 1 and c < slabs - 2:
                hear(c)
                if c + 1 < slabs - 2:
                    tell(c + 1)
            if s < STEPS - 1:
                step_outside(s, cut)
                for later in chunks[s + 1]:
                    if a <= later[0] < a + n:
                        for_sides("rows", lambda side: z_copy(s + 1, side, later).start())
                step_inside(s, cut)
                if c == 0:
                    @pl.when(has["cols"][0])
                    def _():
                        x_copy(s + 1, 0).start()
                if a + n == I:
                    @pl.when(has["cols"][1])
                    def _():
                        x_copy(s + 1, 1).start()

                    for_sides("slabs", lambda side: y_copy(s + 1, side).start())
            else:
                step_inside(s, cut)
                if cut != chunks[s][-1]:
                    step_outside(s, cut)
                    send_sums(early, pl.ds(0, J), cut)
                else:
                    nearer = pl.ds(jnp.where(upper_core, 0, 1), J - 1)
                    step_outside(s, cut, lambda: send_sums(early, nearer, cut))
                    send_sums(late, pl.ds(far, 1), cut)

    tail = chunks[-1][-1]
    eight = pl.ds(0, 8)
    soon = even.at[0, pl.ds(0, 2 * (J * I - tail[1]) // 8), eight]
    for d in range(1, slabs):
        pltpu.make_async_remote_copy(
            soon, soon, s_send, s_recv.at[early, d - 1],
            device_id={"slabs": lax.rem(slab + d, slabs)}, device_id_type=MESH).wait_recv()
    finish((0, J), (0, tail[0]))
    finish((jnp.where(upper_core, 0, 1), jnp.where(upper_core, J - 1, J)), tail)
    for d in range(1, slabs):
        s_copy(late, d, pl.ds(far, 1), tail).wait_recv()
    finish((far, far + 1), tail)

    def all_left(ref, send, axis, side):
        pltpu.make_async_remote_copy(
            ref, ref, send, s_recv.at[0, 0],
            device_id={axis: beside[axis][side]}, device_id_type=MESH).wait_send()

    for_sides("rows", lambda side: all_left(speed.at[pl.ds(0, STEPS)], z_send.at[side], "rows", side))
    for_sides("cols", lambda side: all_left(speed.at[:, pl.ds(0, STEPS)], x_send.at[side], "cols", side))
    for_sides("slabs", lambda side: all_left(speed.at[:, :, pl.ds(0, STEPS)], y_send.at[side], "slabs", side))
    pltpu.make_async_remote_copy(
        stats.at[pl.ds(0, slabs - 1)], stats.at[pl.ds(0, slabs - 1)], s_send, s_recv.at[0, 0],
        device_id={"slabs": lax.rem(slab + 1, slabs)}, device_id_type=MESH).wait_send()


def write_kernel(shape, pieces, last, lines, scaled_hbm, end_hbm, scaled, sems):
    J, I, K, M = shape
    n = I // pieces

    @pl.loop(0, pieces)
    def _(c):
        span = pl.ds(c * n, n)
        pltpu.make_async_copy(last.at[:, span], end_hbm.at[:, span], sems.at[0]).start()

    @pl.loop(0, pieces)
    def _(c):
        @pl.loop(0, n)
        def _(r):
            i = c * n + r
            for j in range(J):
                at = pl.ds(i, 1)
                scaled[j, i] = (last[j, i] - lines[0, j, at]) * lines[1, j, at]

        span = pl.ds(c * n, n)
        pltpu.make_async_copy(scaled.at[:, span], scaled_hbm.at[:, span], sems.at[1]).start()

    pltpu.make_async_copy(last, end_hbm, sems.at[0]).wait()
    pltpu.make_async_copy(scaled, scaled_hbm, sems.at[1]).wait()


def shards(sizes, field_now, earlier, speed_square):
    shape = field_now.shape
    J, I, K, M = shape
    slabs = sizes[2]
    hbm = pl.BlockSpec(memory_space=pltpu.HBM)
    vmem = pl.BlockSpec(memory_space=pltpu.VMEM)
    dma = pltpu.SemaphoreType.DMA
    padded = pltpu.VMEM((J + 2, I + 2, K + 2 * PAD, M), F32)
    arrivals = len(chunks_of(I, 1)) + len(chunks_of(I, STEPS - 1))
    last, lines = pl.pallas_call(
        functools.partial(march_kernel, shape, sizes),
        out_shape=(pltpu.VMEM(shape, F32), pltpu.VMEM((2, J, I, M), F32)),
        in_specs=[hbm, hbm, hbm],
        out_specs=(vmem, vmem),
        scratch_shapes=[
            padded,
            padded,
            pltpu.VMEM(shape, F32),
            pltpu.VMEM((slabs, 2, J, I, M), F32),
            dma((1 + len(chunks_of(I, 0)),)),
            dma((2,)),
            dma((2, arrivals)),
            dma((2,)),
            dma((2, 2)),
            dma((2,)),
            dma((2, 2)),
            dma,
            dma((2, slabs - 1)),
            pltpu.SemaphoreType.REGULAR,
            pltpu.SemaphoreType.REGULAR((slabs - 2,)),
        ],
        compiler_params=pltpu.CompilerParams(
            collective_id=0, has_side_effects=True, vmem_limit_bytes=44 * 2**20
        ),
        name="march",
    )(field_now, earlier, speed_square)
    return pl.pallas_call(
        functools.partial(write_kernel, shape, 8),
        out_shape=(jax.ShapeDtypeStruct(shape, F32), jax.ShapeDtypeStruct(shape, F32)),
        in_specs=[vmem, vmem],
        out_specs=(hbm, hbm),
        scratch_shapes=[pltpu.VMEM(shape, F32), dma((2,))],
        compiler_params=pltpu.CompilerParams(vmem_limit_bytes=12 * 2**20),
        name="write",
    )(last, lines)


def solution(mesh):
    placed = P("rows", "cols", "slabs", None)
    sizes = tuple(mesh.shape[a] for a in ("rows", "cols", "slabs"))
    return jax.shard_map(
        functools.partial(shards, sizes),
        mesh=mesh,
        in_specs=(placed, placed, placed),
        out_specs=(placed, placed),
        check_vma=False,
    )
```

time: 208 us -> 83.3 us (0.40)
  other arithmetic: 88.6 us -> 0 us
  Pallas kernels: 0 us -> 82.6 us
  starting transfers between devices: 44.8 us -> 0 us
  waiting for transfers between devices: 39.6 us -> 0 us
  local copies, waits for them, and re-layouts: 21.2 us -> 0 us
  blocking collectives: 10.9 us -> 0 us
    pallas_call x0 -> x2, Pallas kernels: none -> 82.6 us  [the longest x1 76.7 us: shards(): pl.pallas_call(functools.partial(march_kernel, shape, sizes), out_shape=(...]
    add x3 -> x0, other arithmetic: 50.5 us -> none  [the longest x2 50.4 us: march_step(): return 2.0 * middle - before + speed_square * spread]
    ppermute x18 -> x0, starting transfers between devices: 44.8 us -> none  [the longest x9 30.5 us: extended(): lax.ppermute(last, axis, up)]
    ppermute x18 -> x0, waiting for transfers between devices: 39.6 us -> none  [the longest x9 20 us: extended(): lax.ppermute(last, axis, up)]
    reduce_sum x2 -> x0, other arithmetic: 29.3 us -> none  [the longest x1 28.8 us: shards(): jnp.sum(moved, axis=2, keepdims=True)]
    slice x9 -> x0, local copies, waits for them, and re-layouts: 12.5 us -> none  [the longest x8 9.87 us: extended(): last = lax.slice_in_dim(value, length - width, length, axis=dim)]
    all_to_all x1 -> x0, blocking collectives: 10.9 us -> none  [sent_to_all(): lax.all_to_all(jnp.broadcast_to(value[None], (length, *value.shape)), axi...]
    mul x1 -> x0, other arithmetic: 8.85 us -> none  [shards(): scaled_field = centred * lax.rsqrt(line_variance + 0.0001)]
  transfers between devices with their start and end apart: 18 -> 0, of which waited for: 11 -> 0; matrix products, arithmetic and copies ran while one was open for 6% -> 0% of each run, Pallas kernels for 0% -> 0%
where the time goes in v2:
time: 83.3 us; the launch traced here: 83.2 us
  Pallas kernels  82.6 us (99%)
    pallas_call x1, Pallas kernels, shards(): pl.pallas_call(functools.partial(march_kernel, shape, sizes), out_shape=(...  76.7 us
    pallas_call x1, Pallas kernels, shards(): pl.pallas_call(functools.partial(write_kernel, shape, 8), out_shape=(jax....  5.84 us

profile of v2, /device:TPU:1, one launch (start us, length us, event | category | flops | bytes accessed | tf_op | source)
XLA Modules:
  0.0 83.2 jit_solution(2197992534502611150)
XLA Ops:
  0.6 76.7 %march.1 = (f32[4,32,128,128]{3,2,1,0:T(8,128)S(1)}, f32[2,4,32,128]{3,2,1,0:T(8,128)S(1)}) custom-call(f32[4,32,128,128]{3,2,1,0:T(8,128)} %now_hbm.1, f32[4,32,128,128]{3,2,1,0:T(8,128)} %before_hbm.1, f32[4,32,128,128]{3,2,1,0:T(8,128)} %speed_hbm.1), custom_call_target="tpu_custom_call" | custom-call | tf_op jit(solution)/shard_map/march/pallas_call | solution.py:356
  77.4 5.8 %write.1 = (f32[4,32,128,128]{3,2,1,0:T(8,128)}, f32[4,32,128,128]{3,2,1,0:T(8,128)}) custom-call(f32[4,32,128,128]{3,2,1,0:T(8,128)S(1)} %get-tuple-element.4.last, f32[2,4,32,128]{3,2,1,0:T(8,128)S(1)} %get-tuple-element.5.lines), custom_call_target="tpu_custom_call" | custom-call | tf_op jit(solution)/shard_map/write/pallas_call | solution.py:383

commit v3 on v2

--- a/solution.py
+++ b/solution.py
@@ -14,11 +14,10 @@
 
 
 def chunks_of(rows, step):
-    size = max(rows // 4, 2)
-    cut = [(a, size) for a in range(0, rows, size)]
+    half = rows // 2
+    cut = [(0, half), (half, half)]
     if step == STEPS - 1:
-        first, size = cut.pop()
-        cut += [(first, size // 2), (first + size // 2, size // 2)]
+        cut = [(0, half), (half, half // 2), (half + half // 2, half // 4), (half + 3 * half // 4, half // 4)]
     return cut
 
 
@@ -98,17 +97,20 @@
         return pltpu.make_async_copy(
             ref.at[:, pl.ds(a, n)], buffer.at[planes, pl.ds(start + a, n), width], load_sem.at[sem])
 
+    count = len(chunks[0])
+
     def start_loads(c):
-        if c + 1 < len(chunks[0]):
+        if c + 1 < count:
             load(now_hbm, even, c + 1, c + 1).start()
-        if c < len(chunks[0]):
-            load(before_hbm, odd, c, c + 1).start()
-            load(speed_hbm, speed, c, c + 1).start()
+        if c < count:
+            load(before_hbm, odd, c, count + c).start()
+            load(speed_hbm, speed, c, count + c).start()
 
     def wait_loads(c):
-        a, n = chunks[0][c]
-        amount = pl.ds(0, 3 * n if c + 1 < len(chunks[0]) else 2 * n)
-        pltpu.make_async_copy(speed_hbm.at[:, amount], speed.at[:, amount], load_sem.at[c + 1]).wait()
+        if c + 1 < count:
+            load(now_hbm, even, c + 1, c + 1).wait()
+        amount = pl.ds(0, 2 * chunks[0][c][1])
+        pltpu.make_async_copy(speed_hbm.at[:, amount], speed.at[:, amount], load_sem.at[count + c]).wait()
 
     def for_sides(axis, act):
         for side in (0, 1):
@@ -197,7 +199,7 @@
     def step_plane(s, cut, j):
         a, n = cut
 
-        @pl.loop(a, a + n)
+        @pl.loop(a, a + n, unroll=4 if s == STEPS - 1 else None)
         def _(i):
             value = line(s, j, i)
             if s < STEPS - 1:
@@ -269,10 +271,10 @@
                     tell(c + 1)
             if s < STEPS - 1:
                 step_outside(s, cut)
+                step_inside(s, cut)
                 for later in chunks[s + 1]:
                     if a <= later[0] < a + n:
                         for_sides("rows", lambda side: z_copy(s + 1, side, later).start())
-                step_inside(s, cut)
                 if c == 0:
                     @pl.when(has["cols"][0])
                     def _():
@@ -363,7 +365,7 @@
             padded,
             pltpu.VMEM(shape, F32),
             pltpu.VMEM((slabs, 2, J, I, M), F32),
-            dma((1 + len(chunks_of(I, 0)),)),
+            dma((2 * len(chunks_of(I, 0)),)),
             dma((2,)),
             dma((2, arrivals)),
             dma((2,)),
@@ -381,7 +383,7 @@
         name="march",
     )(field_now, earlier, speed_square)
     return pl.pallas_call(
-        functools.partial(write_kernel, shape, 8),
+        functools.partial(write_kernel, shape, 16),
         out_shape=(jax.ShapeDtypeStruct(shape, F32), jax.ShapeDtypeStruct(shape, F32)),
         in_specs=[vmem, vmem],
         out_specs=(hbm, hbm),

time: 83.3 us -> 83.1 us (level)
  no operation moved by 1% of the time
where the time goes in v3:
time: 83.1 us; the launch traced here: 83 us
  Pallas kernels  82.4 us (99%)
    pallas_call x1, Pallas kernels, shards(): pl.pallas_call(functools.partial(march_kernel, shape, sizes), out_shape=(...  76.6 us
    pallas_call x1, Pallas kernels, shards(): pl.pallas_call(functools.partial(write_kernel, shape, 16), out_shape=(jax...  5.81 us

profile of v3, /device:TPU:1, one launch (start us, length us, event | category | flops | bytes accessed | tf_op | source)
XLA Modules:
  0.0 83.0 jit_solution(8628025696925142405)
XLA Ops:
  0.6 76.6 %march.1 = (f32[4,32,128,128]{3,2,1,0:T(8,128)S(1)}, f32[2,4,32,128]{3,2,1,0:T(8,128)S(1)}) custom-call(f32[4,32,128,128]{3,2,1,0:T(8,128)} %now_hbm.1, f32[4,32,128,128]{3,2,1,0:T(8,128)} %before_hbm.1, f32[4,32,128,128]{3,2,1,0:T(8,128)} %speed_hbm.1), custom_call_target="tpu_custom_call" | custom-call | tf_op jit(solution)/shard_map/march/pallas_call | solution.py:358
  77.2 5.8 %write.1 = (f32[4,32,128,128]{3,2,1,0:T(8,128)}, f32[4,32,128,128]{3,2,1,0:T(8,128)}) custom-call(f32[4,32,128,128]{3,2,1,0:T(8,128)S(1)} %get-tuple-element.4.last, f32[2,4,32,128]{3,2,1,0:T(8,128)S(1)} %get-tuple-element.5.lines), custom_call_target="tpu_custom_call" | custom-call | tf_op jit(solution)/shard_map/write/pallas_call | solution.py:385

commit v4 on v3

--- a/solution.py
+++ b/solution.py
@@ -196,6 +196,20 @@
         old = g[1 + j, 1 + i, kk]
         return (2.0 * centre - old) + speed[j, i] * (total - 6.0 * centre)
 
+    def sum_up(value, j, i):
+        mean = jnp.sum(value, axis=0, keepdims=True) * (1.0 / K)
+        away = value - mean
+        stats[slab, 0, j, pl.ds(i, 1)] = mean
+        stats[slab, 1, j, pl.ds(i, 1)] = jnp.sum(away * away, axis=0, keepdims=True)
+
+    def far_line_but_arriving(s, i):
+        f, g = fields[s], fields[(s + 1) % 2]
+        centre = f[1 + far, 1 + i, kk]
+        total = f[jnp.where(upper_core, far, far + 2), 1 + i, kk]
+        total = total + (f[1 + far, i, kk] + f[1 + far, i + 2, kk])
+        total = total + (f[1 + far, 1 + i, pl.ds(PAD - 1, K)] + f[1 + far, 1 + i, pl.ds(PAD + 1, K)])
+        return (2.0 * centre - g[1 + far, 1 + i, kk]) + speed[far, i] * (total - 6.0 * centre)
+
     def step_plane(s, cut, j):
         a, n = cut
 
@@ -206,10 +220,7 @@
                 fields[(s + 1) % 2][1 + j, 1 + i, kk] = value
             else:
                 last[j, i] = value
-                mean = jnp.sum(value, axis=0, keepdims=True) * (1.0 / K)
-                away = value - mean
-                stats[slab, 0, j, pl.ds(i, 1)] = mean
-                stats[slab, 1, j, pl.ds(i, 1)] = jnp.sum(away * away, axis=0, keepdims=True)
+                sum_up(value, j, i)
 
     def step_inside(s, cut):
         @pl.loop(1, J - 1)
@@ -232,9 +243,24 @@
         step_plane(s, cut, J - 1 - far)
         if between is not None:
             between()
+            a, n = cut
+
+            @pl.loop(a, a + n)
+            def _(i):
+                last[far, i] = far_line_but_arriving(s, i)
+
         wait_below(s, cut, lower_core)
         wait_above(s, cut, upper_core)
-        step_plane(s, cut, far)
+        if between is None:
+            step_plane(s, cut, far)
+        else:
+            arrived = jnp.where(upper_core, J + 1, 0)
+
+            @pl.loop(a, a + n, unroll=4)
+            def _(i):
+                value = last[far, i] + speed[far, i] * fields[s][arrived, 1 + i, kk]
+                last[far, i] = value
+                sum_up(value, far, i)
 
     def finish(planes, rows_i):
         @pl.loop(*planes)
@@ -304,10 +330,6 @@
             device_id={"slabs": lax.rem(slab + d, slabs)}, device_id_type=MESH).wait_recv()
     finish((0, J), (0, tail[0]))
     finish((jnp.where(upper_core, 0, 1), jnp.where(upper_core, J - 1, J)), tail)
-    for d in range(1, slabs):
-        s_copy(late, d, pl.ds(far, 1), tail).wait_recv()
-    finish((far, far + 1), tail)
-
     def all_left(ref, send, axis, side):
         pltpu.make_async_remote_copy(
             ref, ref, send, s_recv.at[0, 0],
@@ -319,6 +341,10 @@
     pltpu.make_async_remote_copy(
         stats.at[pl.ds(0, slabs - 1)], stats.at[pl.ds(0, slabs - 1)], s_send, s_recv.at[0, 0],
         device_id={"slabs": lax.rem(slab + 1, slabs)}, device_id_type=MESH).wait_send()
+
+    for d in range(1, slabs):
+        s_copy(late, d, pl.ds(far, 1), tail).wait_recv()
+    finish((far, far + 1), tail)
 
 
 def write_kernel(shape, pieces, last, lines, scaled_hbm, end_hbm, scaled, sems):

time: 83.1 us -> 83.1 us (level)
  no operation moved by 1% of the time
where the time goes in v4:
time: 83.1 us; the launch traced here: 83 us
  Pallas kernels  82.3 us (99%)
    pallas_call x1, Pallas kernels, shards(): pl.pallas_call(functools.partial(march_kernel, shape, sizes), out_shape=(...  76.5 us
    pallas_call x1, Pallas kernels, shards(): pl.pallas_call(functools.partial(write_kernel, shape, 16), out_shape=(jax...  5.81 us

profile of v4, /device:TPU:1, one launch (start us, length us, event | category | flops | bytes accessed | tf_op | source)
XLA Modules:
  0.0 83.0 jit_solution(7928875929404547074)
XLA Ops:
  0.6 76.5 %march.1 = (f32[4,32,128,128]{3,2,1,0:T(8,128)S(1)}, f32[2,4,32,128]{3,2,1,0:T(8,128)S(1)}) custom-call(f32[4,32,128,128]{3,2,1,0:T(8,128)} %now_hbm.1, f32[4,32,128,128]{3,2,1,0:T(8,128)} %before_hbm.1, f32[4,32,128,128]{3,2,1,0:T(8,128)} %speed_hbm.1), custom_call_target="tpu_custom_call" | custom-call | tf_op jit(solution)/shard_map/march/pallas_call | solution.py:384
  77.1 5.8 %write.1 = (f32[4,32,128,128]{3,2,1,0:T(8,128)}, f32[4,32,128,128]{3,2,1,0:T(8,128)}) custom-call(f32[4,32,128,128]{3,2,1,0:T(8,128)S(1)} %get-tuple-element.4.last, f32[2,4,32,128]{3,2,1,0:T(8,128)S(1)} %get-tuple-element.5.lines), custom_call_target="tpu_custom_call" | custom-call | tf_op jit(solution)/shard_map/write/pallas_call | solution.py:411

commit v5 on v4

--- a/solution.py
+++ b/solution.py
@@ -409,7 +409,7 @@
         name="march",
     )(field_now, earlier, speed_square)
     return pl.pallas_call(
-        functools.partial(write_kernel, shape, 16),
+        functools.partial(write_kernel, shape, 8),
         out_shape=(jax.ShapeDtypeStruct(shape, F32), jax.ShapeDtypeStruct(shape, F32)),
         in_specs=[vmem, vmem],
         out_specs=(hbm, hbm),

time: 83.1 us -> 83.1 us (level)
  no operation moved by 1% of the time
where the time goes in v5:
time: 83.1 us; the launch traced here: 83 us
  Pallas kernels  82.3 us (99%)
    pallas_call x1, Pallas kernels, shards(): pl.pallas_call(functools.partial(march_kernel, shape, sizes), out_shape=(...  76.5 us
    pallas_call x1, Pallas kernels, shards(): pl.pallas_call(functools.partial(write_kernel, shape, 8), out_shape=(jax....  5.84 us

profile of v5, /device:TPU:1, one launch (start us, length us, event | category | flops | bytes accessed | tf_op | source)
XLA Modules:
  0.0 83.0 jit_solution(15600430251149930155)
XLA Ops:
  0.6 76.5 %march.1 = (f32[4,32,128,128]{3,2,1,0:T(8,128)S(1)}, f32[2,4,32,128]{3,2,1,0:T(8,128)S(1)}) custom-call(f32[4,32,128,128]{3,2,1,0:T(8,128)} %now_hbm.1, f32[4,32,128,128]{3,2,1,0:T(8,128)} %before_hbm.1, f32[4,32,128,128]{3,2,1,0:T(8,128)} %speed_hbm.1), custom_call_target="tpu_custom_call" | custom-call | tf_op jit(solution)/shard_map/march/pallas_call | solution.py:384
  77.1 5.8 %write.1 = (f32[4,32,128,128]{3,2,1,0:T(8,128)}, f32[4,32,128,128]{3,2,1,0:T(8,128)}) custom-call(f32[4,32,128,128]{3,2,1,0:T(8,128)S(1)} %get-tuple-element.4.last, f32[2,4,32,128]{3,2,1,0:T(8,128)S(1)} %get-tuple-element.5.lines), custom_call_target="tpu_custom_call" | custom-call | tf_op jit(solution)/shard_map/write/pallas_call | solution.py:411
